TPU v7x, 32 devices: a whole 2x2x4 slice. The times are simulated.
32 devices in a mesh: grp: 2 (over x), kv: 16 (over z, y, core).
Axes of the slice: x: 2, y: 2, z: 4, core: 2. Of those that a mesh axis runs over, the one named last changes fastest.
Arguments:
- queries: bfloat16 [128, 40, 128], P(('grp', 'kv')), parts along dimension 0, may hold values from -250 to 250
- cache_keys: bfloat16 [8192, 40, 128], P(('grp', 'kv')), parts along dimension 0, may hold values from -8 to 8
- cache_values: bfloat16 [8192, 40, 128], P(('grp', 'kv')), parts along dimension 0, may hold values from -18 to 18
- new_keys: bfloat16 [128, 40, 128], P(('grp', 'kv')), parts along dimension 0, may hold values from -4 to 4
- new_values: bfloat16 [128, 40, 128], P(('grp', 'kv')), parts along dimension 0, may hold values from -4 to 4
- valid_frames: int32 [2], P('grp'), parts along dimension 0, may hold values from 8 to 16
Outputs:
- attended: bfloat16 [128, 40, 128], P(('grp', 'kv')), parts along dimension 0
There are 2 independent parts, one for each index of `grp`. A program takes and returns all parts, laid end to end along the dimension named above; each array names one. Nothing has to cross between parts.
All inputs are finite; a program needn't handle non-finite values.
Results may differ from a plain program's by a relative error of at most 0.0027.
Values may be sent and summed in bfloat16 or wider, within the bound.
A program may use at most 128 MiB of HBM per device.

v0:
```python
import math

import jax
import jax.numpy as jnp
from jax import lax
from jax.sharding import PartitionSpec as P

FRAME = 256
QUERY_SPLIT = 4


masked_score = -1e30


def per_device(queries, cache_keys, cache_values, new_keys, new_values, valid_frames):
    q_dev, heads, head_dim = queries.shape
    cache_dev = cache_keys.shape[0]
    factor = 1.0 / math.sqrt(head_dim)
    gathered = lax.all_gather(queries, "kv", axis=0, tiled=True)
    devices = lax.axis_size("kv")
    position = lax.axis_index("kv") * cache_dev + lax.iota(jnp.int32, cache_dev)
    live = position < valid_frames[0] * FRAME
    per_block = q_dev // QUERY_SPLIT
    blocked = gathered.reshape(devices, QUERY_SPLIT, per_block, heads, head_dim)
    pieces = []
    half = heads // 2
    for index in range(QUERY_SPLIT):
        block = blocked[:, index].reshape(devices * per_block, heads, head_dim)
        halves = []
        for which in range(2):
            lower = which * half
            sub_block = block[:, lower : lower + half]
            ckeys = cache_keys[:, lower : lower + half]
            nkeys = new_keys[:, lower : lower + half]
            block_cache_score = (
                jnp.einsum("qhd,khd->hqk", sub_block, ckeys, preferred_element_type=jnp.float32)
                * factor
            )
            block_cache_score = jnp.where(
                live[None, None, :], block_cache_score, jnp.float32(masked_score)
            )
            block_new_score = (
                jnp.einsum("qhd,khd->hqk", sub_block, nkeys, preferred_element_type=jnp.float32)
                * factor
            )
            top = lax.pmax(
                jnp.maximum(jnp.max(block_cache_score, axis=2), jnp.max(block_new_score, axis=2)),
                "kv",
            )
            cache_weight = jnp.exp(block_cache_score - top[:, :, None])
            new_weight = jnp.exp(block_new_score - top[:, :, None])
            total = jnp.sum(cache_weight, axis=2) + jnp.sum(new_weight, axis=2)
            numerator = jnp.einsum(
                "hqk,khd->qhd",
                cache_weight.astype(jnp.bfloat16),
                cache_values[:, lower : lower + half],
                preferred_element_type=jnp.float32,
            )
            numerator = numerator + jnp.einsum(
                "hqk,khd->qhd",
                new_weight.astype(jnp.bfloat16),
                new_values[:, lower : lower + half],
                preferred_element_type=jnp.float32,
            )
            numerator, total = (numerator, total.T)
            summed, denominator = (
                lax.psum_scatter(numerator, "kv", scatter_dimension=0, tiled=True),
                lax.psum_scatter(total, "kv", scatter_dimension=0, tiled=True),
            )
            halves.append((summed / denominator[:, :, None]).astype(jnp.bfloat16))
        pieces.append(jnp.concatenate(halves, axis=1))
    return jnp.concatenate(pieces, axis=0)


def solution(mesh):
    placed = (
        P(("grp", "kv"), None, None),
        P(("grp", "kv"), None, None),
        P(("grp", "kv"), None, None),
        P(("grp", "kv"), None, None),
        P(("grp", "kv"), None, None),
        P("grp"),
    )
    return jax.shard_map(
        per_device,
        mesh=mesh,
        in_specs=placed,
        out_specs=P(("grp", "kv"), None, None),
        check_vma=False,
    )
```

profile of v0, /device:TPU:0, one launch (start us, length us, event | category | flops | bytes accessed | tf_op | source)
XLA Modules:
  0.0 243.8 jit_solution(5140261991207701592)
XLA Ops:
  7.2 25.4 %all_gather.3 = bf16[64,40,128]{2,1,0:T(8,128)(2,1)S(1)} all-gather(bf16[4,40,128]{2,1,0:T(8,128)(2,1)} %param.6), channel_id=1, replica_groups=mesh['grp'=2,'kv'=16] {'kv'}, dimensions={0}, use_global_device_ids=true | all-gather | bytes 696320 | tf_op jit(solution)/shard_map/all_gather | solution.py:19
  33.4 2.8 %fusion.137 = (bf16[256,20,128]{2,1,0:T(8,128)(2,1)S(1)}, bf16[256,20,128]{2,1,0:T(8,128)(2,1)S(1)}) fusion(bf16[256,40,128]{2,1,0:T(8,128)(2,1)} %param.7), kind=kLoop, calls=%fused_computation.191 | loop fusion | bytes 5242880 | tf_op jit(solution)/shard_map/slice | solution.py:33
  37.0 1.2 fusion.155
  39.5 1.2 fusion.153
  40.7 1.2 fusion.149
  43.5 1.2 fusion.147
  45.5 1.2 fusion.145
  47.5 1.2 fusion.143
  49.4 1.2 fusion.141
  57.1 59.8 %all-reduce.18 = (f32[20,16]{1,0:T(8,128)S(1)}, f32[20,16]{1,0:T(8,128)S(1)}, f32[20,16]{1,0:T(8,128)}, f32[20,16]{1,0:T(8,128)}, f32[20,16]{1,0:T(8,128)}, /*in...) all-reduce(f32[20,16]{1,0:T(8,128)} %max.47, ...), channel_id=1, replica_groups=mesh['grp'=2,'kv'=16] {'kv'}, use_global_device_ids=true, to_apply=%region_51.52 | all-reduce | flops 2560 | bytes 20480 | tf_op jit(solution)/shard_map/pmax | solution.py:46
  119.0 2.0 fusion.15
  122.5 1.0 fusion.14
  124.8 1.0 fusion.11
  127.3 1.0 fusion.9
  133.1 58.3 %all-reduce.16 = (f32[16,20]{1,0:T(8,128)S(1)}, f32[16,20]{1,0:T(8,128)S(1)}, f32[16,20]{1,0:T(8,128)S(1)}, f32[16,20]{1,0:T(8,128)S(1)}, f32[16,20]{1,0:T(8,128...) all-reduce(f32[16,20]{1,0:T(8,128)S(1)} %copy.48, ...), channel_id=17, replica_groups=mesh['grp'=2,'kv'=16] {'kv'}, use_global_device_ids=true, to_apply=%region_55.56.clone | all-reduce | flops 2560 | bytes 20480
  196.7 26.4 %all-reduce.21.cloned.1.call-done = (f32[16,20,128]{2,0,1:T(8,128)}, f32[16,20,128]{2,0,1:T(8,128)}, f32[16,20,128]{2,0,1:T(8,128)}, f32[16,20,128]{2,0,1:T(8,12...) async-done(((f32[16,20,128]{2,0,1:T(8,128)}, f32[16,20,128]{2,0,1:T(8,128)}, f32[16,20,128]{2,0,1:T(8,128)}, ...) | async-done | bytes 1310736
  223.1 1.6 fusion.104
  224.8 1.6 fusion.105
  226.4 1.6 fusion.106
  228.0 1.6 fusion.107
  229.7 1.6 fusion.108
  231.3 1.6 fusion.109
  232.9 1.6 fusion.110
  234.6 1.6 fusion.111
  (165 shorter events, 30.0 us)
Async XLA Ops:
  6.5 216.6 %all-reduce.21.cloned.1.call-start = ((), (), s32[]{:S(2)}) async-start(), calls=%async_computation | async-start | bytes 2621440
  33.4 3.6 %copy-start.28 = (bf16[16,1,1,40,128]{4,3,1,0,2:T(8,128)(2,1)}, bf16[16,1,1,40,128]{4,3,1,0,2:T(8,128)(2,1)S(1)}, u32[]{:S(2)}) copy-start(bf16[16,1,1,40,128]{4,3,1,0,2:T(8,128)(2,1)S(1)} %get-tuple-element.33) | copy-start | bytes 491524
  33.4 2.8 %copy-start.44 = (bf16[4,40,128]{2,1,0:T(8,128)(2,1)S(1)}, bf16[4,40,128]{2,1,0:T(8,128)(2,1)}, u32[]{:S(2)}) copy-start(bf16[4,40,128]{2,1,0:T(8,128)(2,1)} %param.9) | copy-start | bytes 122884
  40.7 2.8 %copy-start.26 = (bf16[16,1,1,40,128]{4,3,1,0,2:T(8,128)(2,1)S(1)}, bf16[16,1,1,40,128]{4,3,1,0,2:T(8,128)(2,1)}, u32[]{:S(2)}) copy-start(bf16[16,1,1,40,128]{4,3,1,0,2:T(8,128)(2,1)} %get-tuple-element.34) | copy-start | bytes 491524
  45.5 2.0 copy-start.25
  49.4 2.0 copy-start.45
  49.4 2.0 copy-start
  116.9 4.1 %copy-start.20 = (f32[20,16]{1,0:T(8,128)S(1)}, f32[20,16]{1,0:T(8,128)}, u32[]{:S(2)}) copy-start(f32[20,16]{1,0:T(8,128)} %get-tuple-element.26) | copy-start | bytes 3844
  119.0 3.1 %copy-start.22 = (f32[20,16]{1,0:T(8,128)S(1)}, f32[20,16]{1,0:T(8,128)}, u32[]{:S(2)}) copy-start(f32[20,16]{1,0:T(8,128)} %get-tuple-element.27) | copy-start | bytes 3844
  119.0 3.1 %copy-start.42 = (f32[20,16,4]{1,2,0:T(4,128)S(1)}, f32[20,16,4]{1,2,0:T(4,128)}, u32[]{:S(2)}) copy-start(f32[20,16,4]{1,2,0:T(4,128)} %get-tuple-element.68) | copy-start | bytes 15364
  121.0 1.5 copy-start.10
  122.0 1.5 copy-start.2
  122.5 2.1 copy-start.16
  122.5 2.0 copy-start.32
  124.5 1.5 copy-start.8
  125.8 1.5 copy-start.6
  127.1 1.5 copy-start.12
  129.7 1.4 copy-start.5
  129.7 1.4 copy-start.9
  129.8 1.6 copy-start.35
  129.8 1.6 copy-start.41
  129.8 1.7 copy-start.7
  129.8 1.7 copy-start.13
  130.5 2.0 copy-start.46
  (24 other events, 28.2 us)
Sparse Core Ops, SparseCore 0:
  129.8 93.2 all-reduce.20
where the time goes:
time: 245 us; the launch traced here: 244 us
  blocking collectives  143 us (58%)
  matrix products  27.6 us (11%)
  waiting for transfers between devices  26.5 us (11%)
  other arithmetic  19.4 us (8%)
  between operations  14.7 us (6%)
  local copies, waits for them, and re-layouts  12.2 us (5%)
    pmax x1, blocking collectives, per_device(): lax.pmax(jnp.maximum(jnp.max(block_cache_score, axis=2), jnp.max(block_ne...  59.8 us
    unnamed x1, blocking collectives  58.3 us
    unnamed x2, waiting for transfers between devices  26.5 us
    all_gather x1, blocking collectives, per_device(): gathered = lax.all_gather(queries, 'kv', axis=0, tiled=True)  25.4 us
    convert_element_type x8, other arithmetic, per_device(): halves.append((summed / denominator[:, :, None]).astype(jnp.bfloat16))  13 us
    dot_general x8, matrix products, per_device(): jnp.einsum('hqk,khd->qhd', cache_weight.astype(jnp.bfloat16), cache_value...  9.1 us
    dot_general x8, matrix products, per_device(): jnp.einsum('qhd,khd->hqk', sub_block, ckeys, preferred_element_type=jnp.f...  8.85 us
    dot_general x8, matrix products, per_device(): jnp.einsum('qhd,khd->hqk', sub_block, nkeys, preferred_element_type=jnp.f...  6.33 us
  transfers between devices with their start and end apart: 1, of which 1 were waited for; matrix products, arithmetic and copies ran while one was open for 3% of the time, Pallas kernels for 0%

commit v1 on v0

v1 whole, which is shorter than its diff:
```python
import functools
import math

import jax
import jax.numpy as jnp
from jax import lax
from jax.experimental import pallas as pl
from jax.experimental.pallas import tpu as pltpu
from jax.sharding import PartitionSpec as P

FRAME = 256
GROUP = 8
LANES = 128
MESH = pl.DeviceIdType.MESH
masked_score = -1e30
F32 = jnp.float32


def round_up(value, unit):
    return (value + unit - 1) // unit * unit


def plane_of(devices):
    chips = devices // 2
    inner = 1
    while (inner * 2) * (inner * 2) <= chips:
        inner *= 2
    return chips // inner, inner


def body(dims, q_ref, ck_ref, cv_ref, nk_ref, nv_ref, vf_ref, out_ref,
         qg, qtmp, kst, vst, tmp, kh, vh, scores, mx, num, crecv, ysum, yrecv, zbuf, zrecv,
         load_sem, q_send, q_recv, mx_send, mx_recv, c_send, c_recv, y_send, y_recv, z_send, z_recv):
    n, outer, inner, groups, q_dev, cache_dev, new_dev, unroll = dims
    rows = n * q_dev
    half = rows // 2
    per_y = half // inner
    keys = kh.shape[1]
    me = lax.axis_index("kv")
    c = lax.rem(me, 2)
    b = lax.rem(me // 2, inner)
    a = me // (2 * inner)

    def index_of(a_at, b_at, c_at):
        return (a_at * inner + b_at) * 2 + c_at

    def slot_of(a_at, b_at, c_at):
        return (c_at * inner + b_at) * outer + a_at

    def turn(base, step, size):
        return lax.rem(base + step, size)

    def remote(src, dst, send, recv, target):
        return pltpu.make_async_remote_copy(
            src_ref=src, dst_ref=dst, send_sem=send, recv_sem=recv,
            device_id={"kv": target}, device_id_type=MESH)

    loads = []
    for g in range(groups):
        for at, (source, target) in enumerate(((ck_ref, kst), (cv_ref, vst))):
            copy = pltpu.make_async_copy(source.at[:, g], target.at[g], load_sem.at[g, at])
            copy.start()
            loads.append(copy)

    barrier = pltpu.get_barrier_semaphore()
    for step in range(1, n):
        pl.semaphore_signal(barrier, inc=1, device_id={"kv": turn(me, step, n)}, device_id_type=MESH)
    pl.semaphore_wait(barrier, n - 1)

    mine = slot_of(a, b, c)
    sent = []

    def push(source, slot, send_at, target):
        copy = remote(source, qg.at[slot], q_send.at[send_at], q_recv.at[slot], target)
        copy.start()
        sent.append(copy)

    def arrived(slot):
        remote(q_ref, qg.at[slot], q_send.at[0], q_recv.at[slot], me).wait_recv()

    inner_base = outer
    core_base = inner_base + outer * inner
    for da in range(1, outer):
        push(q_ref, mine, da, index_of(turn(a, da, outer), b, c))
    for db in range(1, inner):
        push(q_ref, mine, inner_base + db, index_of(a, turn(b, db, inner), c))
    push(q_ref, mine, core_base, index_of(a, b, 1 - c))
    qg[mine] = q_ref[...]

    def relayout(source, fresh, target, g):
        fill = keys - cache_dev - new_dev
        tmp[0 : cache_dev * GROUP] = source[g].astype(F32).reshape(cache_dev * GROUP, LANES)
        tmp[cache_dev * GROUP : (cache_dev + new_dev) * GROUP] = (
            fresh[:, g].astype(F32).reshape(new_dev * GROUP, LANES))
        tmp[(cache_dev + new_dev) * GROUP :] = jnp.zeros((fill * GROUP, LANES), F32)
        for h in range(GROUP):
            target[g * GROUP + h] = tmp[pl.ds(h, keys, stride=GROUP), :].astype(jnp.bfloat16)

    for g in range(groups):
        loads[2 * g].wait()
        relayout(kst, nk_ref, kh, g)

    for da in range(1, outer):
        slot = slot_of(turn(a, da, outer), b, c)
        arrived(slot)
        for db in range(1, inner):
            push(qg.at[slot], slot, inner_base + da * inner + db, index_of(a, turn(b, db, inner), c))
        push(qg.at[slot], slot, core_base + da * inner, index_of(a, b, 1 - c))
    for da in range(outer):
        for db in range(1, inner):
            slot = slot_of(turn(a, da, outer), turn(b, db, inner), c)
            arrived(slot)
            push(qg.at[slot], slot, core_base + da * inner + db, index_of(a, b, 1 - c))

    for g in range(groups):
        loads[2 * g + 1].wait()
        relayout(vst, nv_ref, vh, g)

    for da in range(outer):
        for db in range(inner):
            arrived(slot_of(turn(a, da, outer), turn(b, db, inner), 1 - c))

    factor = 1.0 / math.sqrt(LANES)
    lane = lax.broadcasted_iota(jnp.int32, (rows, LANES), 1)
    key_at = lax.broadcasted_iota(jnp.int32, (rows, keys), 1)
    bound = vf_ref[0] * FRAME - me * cache_dev
    live = jnp.logical_or(
        jnp.logical_and(key_at < cache_dev, key_at < bound),
        jnp.logical_and(key_at >= cache_dev, key_at < cache_dev + new_dev))
    wide = mx.shape[3]

    def score_phase(g):
        qtmp[...] = qg[:, :, g].astype(F32).reshape(rows * GROUP, LANES)

        def head(h, best):
            query = qtmp[pl.ds(h, rows, stride=GROUP), :].astype(jnp.bfloat16)
            score = lax.dot_general(
                query, kh[g * GROUP + h], (((1,), (1,)), ((), ())), preferred_element_type=F32) * factor
            score = jnp.where(live, score, F32(masked_score))
            scores[g * GROUP + h] = score
            return jnp.where(lane == h, jnp.max(score, axis=1, keepdims=True), best)

        best = lax.fori_loop(0, GROUP, head, jnp.zeros((rows, LANES), F32), unroll=unroll)
        if wide > rows:
            best = jnp.concatenate([best, jnp.zeros((wide - rows, LANES), F32)], axis=0)
        mx[g, me] = best.T[0:GROUP]
        for step in range(1, n):
            copy = remote(mx.at[g, me], mx.at[g, me], mx_send.at[g, step], mx_recv.at[g, n - step],
                          turn(me, step, n))
            copy.start()
            sent.append(copy)

    def weight_phase(g):
        for step in range(1, n):
            source = turn(me, step, n)
            remote(mx.at[g, me], mx.at[g, source], mx_send.at[g, 0], mx_recv.at[g, step], me).wait_recv()
        top = jnp.max(mx[g], axis=0)
        top = jnp.concatenate([top, jnp.zeros((LANES - GROUP, wide), F32)], axis=0).T[0:rows]

        def head(h, sums):
            column = jnp.max(jnp.where(lane == h, top, -jnp.inf), axis=1, keepdims=True)
            weight = jnp.exp(scores[g * GROUP + h] - column)
            num[g, h] = jnp.dot(weight.astype(jnp.bfloat16), vh[g * GROUP + h], preferred_element_type=F32)
            return jnp.where(lane == h, jnp.sum(weight, axis=1, keepdims=True), sums)

        num[g, GROUP] = lax.fori_loop(0, GROUP, head, jnp.zeros((rows, LANES), F32), unroll=unroll)
        other = pl.ds(pl.multiple_of((1 - c) * half, 8), half)
        copy = remote(num.at[g, :, other], crecv.at[g], c_send.at[g], c_recv.at[g], index_of(a, b, 1 - c))
        copy.start()
        sent.append(copy)

    def core_phase(g):
        remote(crecv.at[g], crecv.at[g], c_send.at[g], c_recv.at[g], me).wait_recv()
        own = pl.ds(pl.multiple_of(c * half, 8), half)
        ysum[g] = num[g, :, own] + crecv[g]
        for db in range(1, inner):
            b_at = turn(b, db, inner)
            part = pl.ds(pl.multiple_of(b_at * per_y, 8), per_y)
            copy = remote(ysum.at[g, :, part], yrecv.at[g, inner - db], y_send.at[g, db],
                          y_recv.at[g, inner - db], index_of(a, b_at, c))
            copy.start()
            sent.append(copy)

    def inner_phase(g):
        part = pl.ds(pl.multiple_of(b * per_y, 8), per_y)
        total = ysum[g, :, part]
        for db in range(1, inner):
            remote(yrecv.at[g, db], yrecv.at[g, db], y_send.at[g, db], y_recv.at[g, db], me).wait_recv()
            total = total + yrecv[g, db]
        for at in range(outer):
            zbuf[g, at] = total[:, at * q_dev : (at + 1) * q_dev]
        for da in range(1, outer):
            a_at = turn(a, da, outer)
            copy = remote(zbuf.at[g, a_at], zrecv.at[g, outer - da], z_send.at[g, da],
                          z_recv.at[g, outer - da], index_of(a_at, b, c))
            copy.start()
            sent.append(copy)

    def outer_phase(g):
        total = zbuf[g, a]
        for da in range(1, outer):
            remote(zrecv.at[g, da], zrecv.at[g, da], z_send.at[g, da], z_recv.at[g, da], me).wait_recv()
            total = total + zrecv[g, da]
        for h in range(GROUP):
            out_ref[g, h] = total[h] / total[GROUP][:, h : h + 1]

    for g in range(groups):
        score_phase(g)
    stages = (weight_phase, core_phase, inner_phase, outer_phase)
    for step in range(groups + len(stages) - 1):
        for depth, stage in enumerate(stages):
            if 0 <= step - depth < groups:
                stage(step - depth)
    for copy in sent:
        copy.wait_send()


def attend(number, queries, cache_keys, cache_values, new_keys, new_values, valid_frames):
    n = lax.axis_size("kv")
    outer, inner = plane_of(n)
    q_dev, groups = queries.shape[:2]
    cache_dev, new_dev = cache_keys.shape[0], new_keys.shape[0]
    rows = n * q_dev
    half = rows // 2
    per_y = half // inner
    keys = cache_dev + round_up(new_dev, 16)
    slots = GROUP + 1
    wide = round_up(rows, LANES)
    unroll = GROUP if rows <= LANES else 1
    dims = (n, outer, inner, groups, q_dev, cache_dev, new_dev, unroll)
    bf16 = jnp.bfloat16
    vmem = pl.BlockSpec(memory_space=pltpu.VMEM)
    hbm = pl.BlockSpec(memory_space=pl.ANY)
    dma = pltpu.SemaphoreType.DMA
    return pl.pallas_call(
        functools.partial(body, dims),
        out_shape=jax.ShapeDtypeStruct((groups, GROUP, q_dev, LANES), F32),
        in_specs=[vmem, hbm, hbm, vmem, vmem, pl.BlockSpec(memory_space=pltpu.SMEM)],
        out_specs=vmem,
        scratch_shapes=[
            pltpu.VMEM((n, q_dev, groups, GROUP, LANES), bf16),
            pltpu.VMEM((rows * GROUP, LANES), F32),
            pltpu.VMEM((groups, cache_dev, GROUP, LANES), bf16),
            pltpu.VMEM((groups, cache_dev, GROUP, LANES), bf16),
            pltpu.VMEM((keys * GROUP, LANES), F32),
            pltpu.VMEM((groups * GROUP, keys, LANES), bf16),
            pltpu.VMEM((groups * GROUP, keys, LANES), bf16),
            pltpu.VMEM((groups * GROUP, rows, keys), F32),
            pltpu.VMEM((groups, n, GROUP, wide), F32),
            pltpu.VMEM((groups, slots, rows, LANES), F32),
            pltpu.VMEM((groups, slots, half, LANES), F32),
            pltpu.VMEM((groups, slots, half, LANES), F32),
            pltpu.VMEM((groups, inner, slots, per_y, LANES), F32),
            pltpu.VMEM((groups, outer, slots, q_dev, LANES), F32),
            pltpu.VMEM((groups, outer, slots, q_dev, LANES), F32),
            dma((groups, 2)),
            dma((outer + 2 * outer * inner,)),
            dma((n,)),
            dma((groups, n)),
            dma((groups, n)),
            dma((groups,)),
            dma((groups,)),
            dma((groups, inner)),
            dma((groups, inner)),
            dma((groups, outer)),
            dma((groups, outer)),
        ],
        compiler_params=pltpu.CompilerParams(
            collective_id=number, has_side_effects=True, vmem_limit_bytes=62 * 1024 * 1024),
    )(queries, cache_keys, cache_values, new_keys, new_values, valid_frames)


def per_device(queries, cache_keys, cache_values, new_keys, new_values, valid_frames):
    q_dev, heads, head_dim = queries.shape
    groups = heads // GROUP
    arrays = [x.reshape(x.shape[0], groups, GROUP, head_dim)
              for x in (queries, cache_keys, cache_values, new_keys, new_values)]
    calls = 1 if lax.axis_size("kv") * q_dev <= LANES else groups
    size = groups // calls
    parts = [
        attend(at, *[x[:, at * size : (at + 1) * size] for x in arrays], valid_frames)
        for at in range(calls)
    ]
    result = parts[0] if calls == 1 else jnp.concatenate(parts, axis=0)
    return result.transpose(2, 0, 1, 3).reshape(q_dev, heads, head_dim).astype(queries.dtype)


def solution(mesh):
    placed = (P(("grp", "kv"), None, None),) * 5 + (P("grp"),)
    return jax.shard_map(
        per_device,
        mesh=mesh,
        in_specs=placed,
        out_specs=P(("grp", "kv"), None, None),
        check_vma=False,
    )
```

time: 245 us -> 47.6 us (0.19)
  blocking collectives: 143 us -> 0 us
  Pallas kernels: 0 us -> 45.2 us
  matrix products: 27.6 us -> 0 us
  waiting for transfers between devices: 26.5 us -> 0 us
  other arithmetic: 19.4 us -> 0.9 us
  between operations: 14.7 us -> 0.66 us
  local copies, waits for them, and re-layouts: 12.2 us -> 0.62 us
    pmax x1 -> x0, blocking collectives: 59.8 us -> none  [per_device(): lax.pmax(jnp.maximum(jnp.max(block_cache_score, axis=2), jnp.max(block_ne...]
    unnamed x1 -> x0, blocking collectives: 58.3 us -> none
    pallas_call x0 -> x1, Pallas kernels: none -> 45.2 us  [attend(): pl.pallas_call(functools.partial(body, dims), out_shape=jax.ShapeDtypeStr...]
    dot_general x32 -> x0, matrix products: 27.6 us -> none  [the longest x8 9.1 us: per_device(): jnp.einsum('hqk,khd->qhd', cache_weight.astype(jnp.bfloat16), cache_value...]
    unnamed x2 -> x0, waiting for transfers between devices: 26.5 us -> none
    all_gather x1 -> x0, blocking collectives: 25.4 us -> none  [per_device(): gathered = lax.all_gather(queries, 'kv', axis=0, tiled=True)]
    convert_element_type x8 -> x1, other arithmetic: 13 us -> 0.9 us  [per_device(): result.transpose(2, 0, 1, 3).reshape(q_dev, heads, head_dim)]
    div x8 -> x0, local copies, waits for them, and re-layouts: 5.23 us -> none  [per_device(): halves.append((summed / denominator[:, :, None]).astype(jnp.bfloat16))]
  transfers between devices with their start and end apart: 1 -> 0, of which waited for: 1 -> 0; matrix products, arithmetic and copies ran while one was open for 3% -> 0% of each run, Pallas kernels for 0% -> 0%
where the time goes in v1:
time: 47.6 us; the launch traced here: 47.4 us
  Pallas kernels  45.2 us (95%)
  other arithmetic  0.9 us (2%)
  between operations  0.66 us (1%)
  local copies, waits for them, and re-layouts  0.62 us (1%)
    pallas_call x1, Pallas kernels, attend(): pl.pallas_call(functools.partial(body, dims), out_shape=jax.ShapeDtypeStr...  45.2 us

profile of v1, /device:TPU:0, one launch (start us, length us, event | category | flops | bytes accessed | tf_op | source)
XLA Modules:
  0.0 47.4 jit_solution(11499188087971516412)
XLA Ops:
  0.7 45.2 %shard_map.64 = f32[5,8,4,128]{3,2,1,0:T(4,128)} custom-call(bf16[4,5,8,128]{3,2,1,0:T(8,128)(2,1)} %bitcast.11, bf16[256,5,8,128]{3,2,1,0:T(8,128)(2,1)} %bitcast.8, bf16[256,5,8,128]{3,2,1,0:T(8,128)(2,1)} %bitcast.9, bf16[4,5,8,128]{3,2,1,0:T(8,128)(2,1)} %bitcast.12, bf16[4,5,8,128]{3,2,1,0:T(8,128)(2,1)} %bitcast.13, s32[1]{0:T(128)S(6)} %copy.8.vf_ref), custom_call_target="tpu_custom_call" | custom-call | tf_op jit(solution)/shard_map/pallas_call | solution.py:235
  45.8 0.9 %convert_element_type.9 = bf16[5,8,4,128]{3,2,1,0:T(4,128)(2,1)S(1)} convert(f32[5,8,4,128]{3,2,1,0:T(4,128)} %shard_map.64) | non-fusion elementwise | flops 20480 | bytes 122880 | tf_op jit(solution)/shard_map/convert_element_type | solution.py:285
  46.7 0.6 %copy.7 = bf16[4,40,128]{2,1,0:T(8,128)(2,1)} copy(bf16[4,40,128]{2,0,1:T(4,128)(2,1)S(1)} %bitcast.10) | data formatting | bytes 81920 | tf_op jit(solution)/shard_map/convert_element_type | solution.py:285

commit v2 on v1

v2 whole, which is shorter than its diff:
```python
import functools
import math

import jax
import jax.numpy as jnp
from jax import lax
from jax.experimental import pallas as pl
from jax.experimental.pallas import tpu as pltpu
from jax.sharding import PartitionSpec as P

FRAME = 256
GROUP = 8
LOADS = 4
LAGS = (0, 1, 4, 8)
LANES = 128
MESH = pl.DeviceIdType.MESH
masked_score = -1e30
F32 = jnp.float32


def round_up(value, unit):
    return (value + unit - 1) // unit * unit


def plane_of(devices):
    chips = devices // 2
    inner = 1
    while (inner * 2) * (inner * 2) <= chips:
        inner *= 2
    return chips // inner, inner


def body(dims, q_hbm, ck_ref, cv_ref, nk_hbm, nv_hbm, vf_hbm, out_ref,
         q_ref, nk_ref, nv_ref, vf_ref, small_sem,
         qg, qtmp, kst, vst, tmp, kh, vh, scores, mx, num, crecv, ysum, yrecv, zbuf, zrecv,
         load_sem, q_send, q_recv, mx_send, mx_recv, c_send, c_recv, y_send, y_recv, z_send, z_recv):
    n, outer, inner, cuts, q_dev, cache_dev, new_dev, unroll, pack = dims
    groups = cuts[-1]
    rows = n * q_dev
    half = rows // 2
    per_y = half // inner
    keys = kh.shape[1]
    me = lax.axis_index("kv")
    c = lax.rem(me, 2)
    b = lax.rem(me // 2, inner)
    a = me // (2 * inner)

    def index_of(a_at, b_at, c_at):
        return (a_at * inner + b_at) * 2 + c_at

    def slot_of(a_at, b_at, c_at):
        return (c_at * inner + b_at) * outer + a_at

    def turn(base, step, size):
        return lax.rem(base + step, size)

    def remote(src, dst, send, recv, target):
        return pltpu.make_async_remote_copy(
            src_ref=src, dst_ref=dst, send_sem=send, recv_sem=recv,
            device_id={"kv": target}, device_id_type=MESH)

    small = [
        pltpu.make_async_copy(source, target, small_sem.at[at])
        for at, (source, target) in enumerate(
            ((q_hbm, q_ref), (nk_hbm, nk_ref), (nv_hbm, nv_ref), (vf_hbm, vf_ref)))
    ]
    for copy in small:
        copy.start()
    loads = []
    for at, (source, target) in enumerate(((ck_ref, kst), (cv_ref, vst))):
        for part in range(LOADS):
            span = pl.ds(part * (cache_dev // LOADS), cache_dev // LOADS)
            copy = pltpu.make_async_copy(source.at[span], target.at[span], load_sem.at[at, part])
            copy.start()
            loads.append(copy)

    barrier = pltpu.get_barrier_semaphore()
    partners = [index_of(turn(a, da, outer), b, c) for da in range(1, outer)]
    partners += [index_of(a, turn(b, db, inner), c) for db in range(1, inner)]
    partners.append(index_of(a, b, 1 - c))
    for partner in partners:
        pl.semaphore_signal(barrier, inc=1, device_id={"kv": partner}, device_id_type=MESH)
    pl.semaphore_wait(barrier, len(partners))
    small[0].wait()

    mine = slot_of(a, b, c)
    sent = []

    def push(source, slot, piece, send_at, target):
        span = pl.ds(cuts[piece], cuts[piece + 1] - cuts[piece])
        copy = remote(source.at[:, span], qg.at[slot, :, span], q_send.at[piece, send_at],
                      q_recv.at[piece, slot], target)
        copy.start()
        sent.append(copy)

    def arrived(slot, piece):
        span = pl.ds(cuts[piece], cuts[piece + 1] - cuts[piece])
        remote(q_ref.at[:, span], qg.at[slot, :, span], q_send.at[piece, 0], q_recv.at[piece, slot],
               me).wait_recv()

    inner_base = outer
    core_base = inner_base + outer * inner
    pieces = len(cuts) - 1
    for piece in range(pieces):
        for da in range(1, outer):
            push(q_ref, mine, piece, da, index_of(turn(a, da, outer), b, c))
        for db in range(1, inner):
            push(q_ref, mine, piece, inner_base + db, index_of(a, turn(b, db, inner), c))
        push(q_ref, mine, piece, core_base, index_of(a, b, 1 - c))
    qg[mine] = q_ref[...]

    def relayout(source, fresh, target, g):
        fill = keys - cache_dev - new_dev
        tmp[0 : cache_dev * GROUP] = source[:, g].astype(F32).reshape(cache_dev * GROUP, LANES)
        tmp[cache_dev * GROUP : (cache_dev + new_dev) * GROUP] = (
            fresh[:, g].astype(F32).reshape(new_dev * GROUP, LANES))
        tmp[(cache_dev + new_dev) * GROUP :] = jnp.zeros((fill * GROUP, LANES), F32)
        for h in range(GROUP):
            target[g * GROUP + h] = tmp[pl.ds(h, keys, stride=GROUP), :].astype(jnp.bfloat16)

    for copy in small[1:] + loads[:LOADS]:
        copy.wait()
    for g in range(groups):
        relayout(kst, nk_ref, kh, g)

    def forward_outer(piece):
        for da in range(1, outer):
            slot = slot_of(turn(a, da, outer), b, c)
            arrived(slot, piece)
            for db in range(1, inner):
                push(qg.at[slot], slot, piece, inner_base + da * inner + db,
                     index_of(a, turn(b, db, inner), c))
            push(qg.at[slot], slot, piece, core_base + da * inner, index_of(a, b, 1 - c))

    def forward_inner(piece):
        for da in range(outer):
            for db in range(1, inner):
                slot = slot_of(turn(a, da, outer), turn(b, db, inner), c)
                arrived(slot, piece)
                push(qg.at[slot], slot, piece, core_base + da * inner + db, index_of(a, b, 1 - c))

    def gathered(piece):
        for da in range(outer):
            for db in range(inner):
                arrived(slot_of(turn(a, da, outer), turn(b, db, inner), 1 - c), piece)

    factor = 1.0 / math.sqrt(LANES)
    lane = lax.broadcasted_iota(jnp.int32, (rows, LANES), 1)
    key_at = lax.broadcasted_iota(jnp.int32, (rows, keys), 1)
    bound = vf_ref[0] * FRAME - me * cache_dev
    live = jnp.logical_or(
        jnp.logical_and(key_at < cache_dev, key_at < bound),
        jnp.logical_and(key_at >= cache_dev, key_at < cache_dev + new_dev))
    tall, wide = mx.shape[2:]

    def score_phase(g):
        qtmp[...] = qg[:, :, g].astype(F32).reshape(rows * GROUP, LANES)

        def head(h, best):
            query = qtmp[pl.ds(h, rows, stride=GROUP), :].astype(jnp.bfloat16)
            score = lax.dot_general(
                query, kh[g * GROUP + h], (((1,), (1,)), ((), ())), preferred_element_type=F32) * factor
            score = jnp.where(live, score, F32(masked_score))
            scores[g * GROUP + h] = score
            return jnp.where(lane == h, jnp.max(score, axis=1, keepdims=True), best)

        best = lax.fori_loop(0, GROUP, head, jnp.zeros((rows, LANES), F32), unroll=unroll)
        if pack > 1:
            best = jnp.concatenate(
                [best] + [pltpu.roll(best, LANES - at * tall, 1) for at in range(1, pack)], axis=0)
        mx[g, me] = best.T[0:tall]
        for step in range(1, n):
            copy = remote(mx.at[g, me], mx.at[g, me], mx_send.at[g, step], mx_recv.at[g, n - step],
                          turn(me, step, n))
            copy.start()
            sent.append(copy)

    totals = [jnp.zeros((rows, LANES), F32)]
    finished = []

    def slots_of(g):
        return pl.ds(0, GROUP + (g == groups - 1))

    def weight_phase(g):
        for step in range(1, n):
            source = turn(me, step, n)
            remote(mx.at[g, me], mx.at[g, source], mx_send.at[g, 0], mx_recv.at[g, step], me).wait_recv()
        top = jnp.max(mx[g], axis=0)
        turned = jnp.concatenate([top, jnp.zeros((LANES - tall, wide), F32)], axis=0).T
        top = turned[0:rows]
        for at in range(1, pack):
            moved = pltpu.roll(turned[at * rows : (at + 1) * rows], at * tall, 1)
            top = jnp.where(lane < at * tall, top, moved)

        def head(h, sums):
            column = jnp.max(jnp.where(lane == h, top, -jnp.inf), axis=1, keepdims=True)
            weight = jnp.exp(scores[g * GROUP + h] - column)
            num[g, h] = jnp.dot(weight.astype(jnp.bfloat16), vh[g * GROUP + h], preferred_element_type=F32)
            return jnp.where(lane == g * GROUP + h, jnp.sum(weight, axis=1, keepdims=True), sums)

        sums = lax.fori_loop(0, GROUP, head, totals[-1], unroll=unroll)
        totals.append(sums)
        if g == groups - 1:
            num[g, GROUP] = sums
        other = pl.ds(pl.multiple_of((1 - c) * half, 8), half)
        copy = remote(num.at[g, slots_of(g), other], crecv.at[g, slots_of(g)], c_send.at[g], c_recv.at[g], index_of(a, b, 1 - c))
        copy.start()
        sent.append(copy)

    def core_phase(g):
        remote(crecv.at[g, slots_of(g)], crecv.at[g, slots_of(g)], c_send.at[g], c_recv.at[g], me).wait_recv()
        own = pl.ds(pl.multiple_of(c * half, 8), half)
        use = slots_of(g)
        ysum[g, use] = num[g, use, own] + crecv[g, use]
        for db in range(1, inner):
            b_at = turn(b, db, inner)
            part = pl.ds(pl.multiple_of(b_at * per_y, 8), per_y)
            copy = remote(ysum.at[g, use, part], yrecv.at[g, inner - db, use], y_send.at[g, db],
                          y_recv.at[g, inner - db], index_of(a, b_at, c))
            copy.start()
            sent.append(copy)

    def inner_phase(g):
        part = pl.ds(pl.multiple_of(b * per_y, 8), per_y)
        use = slots_of(g)
        total = ysum[g, use, part]
        for db in range(1, inner):
            remote(yrecv.at[g, db, use], yrecv.at[g, db, use], y_send.at[g, db], y_recv.at[g, db], me).wait_recv()
            total = total + yrecv[g, db, use]
        for at in range(outer):
            zbuf[g, at, use] = total[:, at * q_dev : (at + 1) * q_dev]
        for da in range(1, outer):
            a_at = turn(a, da, outer)
            copy = remote(zbuf.at[g, a_at, use], zrecv.at[g, outer - da, use], z_send.at[g, da],
                          z_recv.at[g, outer - da], index_of(a_at, b, c))
            copy.start()
            sent.append(copy)

    def outer_phase(g):
        use = slots_of(g)
        total = zbuf[g, a, use]
        for da in range(1, outer):
            remote(zrecv.at[g, da, use], zrecv.at[g, da, use], z_send.at[g, da], z_recv.at[g, da], me).wait_recv()
            total = total + zrecv[g, da, use]
        finished.append(total)
        if g == groups - 1:
            for done in range(groups):
                for h in range(GROUP):
                    at = done * GROUP + h
                    out_ref[:, done, h] = finished[done][h] / total[GROUP][:, at : at + 1]

    for piece in range(pieces):
        forward_outer(piece)
    for piece in range(pieces):
        forward_inner(piece)
        gathered(piece)
        for g in range(cuts[piece], cuts[piece + 1]):
            score_phase(g)
    for copy in loads[LOADS:]:
        copy.wait()
    for g in range(groups):
        relayout(vst, nv_ref, vh, g)
    stages = (weight_phase, core_phase, inner_phase, outer_phase)
    for step in range(groups + LAGS[-1]):
        for lag, stage in zip(LAGS, stages):
            if 0 <= step - lag < groups:
                stage(step - lag)
    for copy in sent:
        copy.wait_send()


def attend(number, queries, cache_keys, cache_values, new_keys, new_values, valid_frames):
    n = lax.axis_size("kv")
    outer, inner = plane_of(n)
    q_dev, groups = queries.shape[:2]
    cache_dev, new_dev = cache_keys.shape[0], new_keys.shape[0]
    rows = n * q_dev
    half = rows // 2
    per_y = half // inner
    keys = cache_dev + round_up(new_dev, 16)
    slots = GROUP + 1
    wide = max(rows, LANES)
    unroll = GROUP if rows <= LANES else 1
    pack = max(LANES // rows, 1)
    cuts = (0, 2, groups) if groups > 2 else (0, groups)
    pieces = len(cuts) - 1
    dims = (n, outer, inner, cuts, q_dev, cache_dev, new_dev, unroll, pack)
    bf16 = jnp.bfloat16
    vmem = pl.BlockSpec(memory_space=pltpu.VMEM)
    hbm = pl.BlockSpec(memory_space=pl.ANY)
    dma = pltpu.SemaphoreType.DMA
    return pl.pallas_call(
        functools.partial(body, dims),
        out_shape=jax.ShapeDtypeStruct((q_dev, groups, GROUP, LANES), F32),
        in_specs=[hbm] * 6,
        out_specs=vmem,
        scratch_shapes=[
            pltpu.VMEM(queries.shape, bf16),
            pltpu.VMEM(new_keys.shape, bf16),
            pltpu.VMEM(new_values.shape, bf16),
            pltpu.SMEM(valid_frames.shape, jnp.int32),
            dma((4,)),
            pltpu.VMEM((n, q_dev, groups, GROUP, LANES), bf16),
            pltpu.VMEM((rows * GROUP, LANES), F32),
            pltpu.VMEM((cache_dev, groups, GROUP, LANES), bf16),
            pltpu.VMEM((cache_dev, groups, GROUP, LANES), bf16),
            pltpu.VMEM((keys * GROUP, LANES), F32),
            pltpu.VMEM((groups * GROUP, keys, LANES), bf16),
            pltpu.VMEM((groups * GROUP, keys, LANES), bf16),
            pltpu.VMEM((groups * GROUP, rows, keys), F32),
            pltpu.VMEM((groups, n, GROUP // pack, wide), F32),
            pltpu.VMEM((groups, slots, rows, LANES), F32),
            pltpu.VMEM((groups, slots, half, LANES), F32),
            pltpu.VMEM((groups, slots, half, LANES), F32),
            pltpu.VMEM((groups, inner, slots, per_y, LANES), F32),
            pltpu.VMEM((groups, outer, slots, q_dev, LANES), F32),
            pltpu.VMEM((groups, outer, slots, q_dev, LANES), F32),
            dma((2, LOADS)),
            dma((pieces, outer + 2 * outer * inner)),
            dma((pieces, n)),
            dma((groups, n)),
            dma((groups, n)),
            dma((groups,)),
            dma((groups,)),
            dma((groups, inner)),
            dma((groups, inner)),
            dma((groups, outer)),
            dma((groups, outer)),
        ],
        compiler_params=pltpu.CompilerParams(
            collective_id=number, has_side_effects=True, vmem_limit_bytes=62 * 1024 * 1024),
    )(queries, cache_keys, cache_values, new_keys, new_values, valid_frames)


def per_device(queries, cache_keys, cache_values, new_keys, new_values, valid_frames):
    q_dev, heads, head_dim = queries.shape
    groups = heads // GROUP
    arrays = [x.reshape(x.shape[0], groups, GROUP, head_dim)
              for x in (queries, cache_keys, cache_values, new_keys, new_values)]
    calls = 1 if lax.axis_size("kv") * q_dev <= LANES else groups
    size = groups // calls
    parts = [
        attend(at, *[x[:, at * size : (at + 1) * size] for x in arrays], valid_frames)
        for at in range(calls)
    ]
    result = parts[0] if calls == 1 else jnp.concatenate(parts, axis=1)
    return result.reshape(q_dev, heads, head_dim).astype(queries.dtype)


def solution(mesh):
    placed = (P(("grp", "kv"), None, None),) * 5 + (P("grp"),)
    return jax.shard_map(
        per_device,
        mesh=mesh,
        in_specs=placed,
        out_specs=P(("grp", "kv"), None, None),
        check_vma=False,
    )
```

time: 47.6 us -> 39.2 us (0.82)
  Pallas kernels: 45.2 us -> 36.9 us
  local copies, waits for them, and re-layouts: 0.62 us -> 0 us
  other arithmetic: 0.9 us -> 1.51 us
    pallas_call x1, Pallas kernels: 45.2 us -> 36.9 us  [attend(): pl.pallas_call(functools.partial(body, dims), out_shape=jax.ShapeDtypeStr...]
    convert_element_type x1 -> x0, local copies, waits for them, and re-layouts: 0.62 us -> none  [per_device(): result.transpose(2, 0, 1, 3).reshape(q_dev, heads, head_dim)]
    convert_element_type x1, other arithmetic: 0.9 us -> 1.51 us  [per_device(): return result.reshape(q_dev, heads, head_dim).astype(queries.dtype)]
where the time goes in v2:
time: 39.2 us; the launch traced here: 39 us
  Pallas kernels  36.9 us (94%)
  other arithmetic  1.51 us (4%)
  between operations  0.66 us (2%)
    pallas_call x1, Pallas kernels, attend(): pl.pallas_call(functools.partial(body, dims), out_shape=jax.ShapeDtypeStr...  36.9 us
    convert_element_type x1, other arithmetic, per_device(): return result.reshape(q_dev, heads, head_dim).astype(queries.dtype)  1.51 us

profile of v2, /device:TPU:0, one launch (start us, length us, event | category | flops | bytes accessed | tf_op | source)
XLA Modules:
  0.0 39.0 jit_solution(7418907076959605614)
XLA Ops:
  0.7 36.9 %shard_map.64 = f32[4,5,8,128]{3,2,1,0:T(8,128)} custom-call(bf16[4,5,8,128]{3,2,1,0:T(8,128)(2,1)} %bitcast.9, bf16[256,5,8,128]{3,2,1,0:T(8,128)(2,1)} %bitcast.7, bf16[256,5,8,128]{3,2,1,0:T(8,128)(2,1)} %bitcast.8, bf16[4,5,8,128]{3,2,1,0:T(8,128)(2,1)} %bitcast.10, bf16[4,5,8,128]{3,2,1,0:T(8,128)(2,1)} %bitcast.11, s32[1]{0:T(128)S(6)} %copy.7.vf_hbm), custom_call_target="tpu_custom_call" | custom-call | tf_op jit(solution)/shard_map/pallas_call | solution.py:292
  37.5 1.5 %convert_bitcast_fusion = bf16[4,40,128]{2,1,0:T(8,128)(2,1)} fusion(f32[4,5,8,128]{3,2,1,0:T(8,128)} %shard_map.64), kind=kLoop, calls=%fused_computation | loop fusion | flops 20480 | bytes 122880 | tf_op jit(solution)/shard_map/convert_element_type | solution.py:347
